TPU v7x, 256 devices: a whole 4x4x8 slice. The times are simulated.
256 devices in a mesh: bx: 16 (over x, y), by: 16 (over z, core).
Axes of the slice: x: 4, y: 4, z: 8, core: 2. Of those that a mesh axis runs over, the one named last changes fastest.
Arguments:
- forcing: float32 [2432, 4096], P('by', 'bx'), may hold values from -20 to 20
- guess: float32 [2432, 4096], P('by', 'bx'), may hold values from -3 to 3
- shift: float32 [2432, 4096], P('by', 'bx'), may hold values from 0.05 to 2
- ocean_mask: int32 [2432, 4096], P('by', 'bx'), may hold values 0 or 1
Outputs:
- solution_field: float32 [2432, 4096], P('by', 'bx')
- residual: float32 [2432, 4096], P('by', 'bx')
- residual_norm: float32 [], replicated
All inputs are finite; a program needn't handle non-finite values. No bound on the sum of `ocean_mask` on one device may be relied on, other than what follows from the above.
Results may differ from a plain program's by a relative error of at most 0.00002.
Values sent between devices are 32-bit elements; how exact they have to be, the bound alone decides.
A program may use at most 64 MiB of HBM per device.

v0:
```python
import jax
import jax.numpy as jnp
from jax import lax
from jax.sharding import PartitionSpec as P

ITERS = 4
LOW_BOUND = 0.05
HIGH_BOUND = 14.5


def padded_2(block, sides, width):
    for axis, dim in sides:
        count = lax.axis_size(axis)
        forward = [(i, i + 1) for i in range(count - 1)]
        forward.append((count - 1, 0))
        backward = [(target, source) for source, target in forward]
        low = lax.ppermute(
            lax.slice_in_dim(block, block.shape[dim] - width, None, axis=dim), axis, forward
        )
        high = lax.ppermute(lax.slice_in_dim(block, 0, width, axis=dim), axis, backward)
        block = jnp.concatenate([low, block, high], axis=dim)
    return block


def sent_to_all(x, axis):
    copies = jnp.broadcast_to(x, (lax.axis_size(axis), *x.shape))
    return lax.all_to_all(copies, axis, split_axis=0, concat_axis=0, tiled=True)


def laid_out(tiles, dim):
    tiles = jnp.moveaxis(tiles, 0, dim)
    dims = tiles.shape
    return tiles.reshape(*dims[:dim], dims[dim] * dims[dim + 1], *dims[dim + 2 :])


def gather_directly(x, axis, dim):
    tiles = sent_to_all(x, axis)
    return laid_out(tiles, dim)


def gather_turned(arrays, axis, dims):
    turned = [jnp.moveaxis(a, dim, 0) for a, dim in zip(arrays, dims)]
    both = jnp.concatenate([t.reshape(len(t), -1) for t in turned], axis=1)
    filled, at, outs = (lax.all_gather(both, axis, axis=0, tiled=True), 0, [])
    for t, dim in zip(turned, dims):
        piece = filled[:, at : at + t[0].size].reshape(-1, *t.shape[1:])
        outs.append(jnp.moveaxis(piece, 0, dim))
        at += t[0].size
    return tuple(outs)


def stencil_padded(padded, shift, mask_f):
    center = padded[1:-1, 1:-1]
    sides = padded[2:, 1:-1] + padded[:-2, 1:-1] + padded[1:-1, 2:] + padded[1:-1, :-2]
    corners = padded[2:, 2:] + padded[2:, :-2] + padded[:-2, 2:] + padded[:-2, :-2]
    return mask_f * ((6.0 + shift) * center - sides - 0.5 * corners)


def crop_cycle(values, cycle):
    return values[cycle : values.shape[0] - cycle, cycle : values.shape[1] - cycle]


def local_stencil(values, shift_full, mask_full):
    cycle = (shift_full.shape[0] - values.shape[0]) // 2 + 1
    return stencil_padded(values, crop_cycle(shift_full, cycle), crop_cycle(mask_full, cycle))


def deep_inputs(forcing, guess, shift, mask_f):
    rows, cols = forcing.shape
    depth = ITERS + 1
    stacked = jnp.stack([forcing, guess, shift, mask_f])
    padded = padded_2(stacked, (("bx", 2), ("by", 1)), depth)
    top_rows = stacked[:, rows - depth :, :]
    whole_top = gather_directly(top_rows, "bx", 2)
    flipped = whole_top[:, ::-1, ::-1]
    extended = jnp.concatenate([flipped[:, :, -depth:], flipped, flipped[:, :, :depth]], axis=2)
    ghost = lax.dynamic_slice_in_dim(extended, lax.axis_index("bx") * cols, cols + 2 * depth, 2)
    row_index = lax.axis_index("by")
    upper_rows = jnp.where(row_index == lax.axis_size("by") - 1, ghost, padded[:, rows + depth :])
    lower_rows = jnp.where(row_index == 0, jnp.zeros_like(ghost), padded[:, :depth])
    return jnp.concatenate([lower_rows, padded[:, depth : rows + depth], upper_rows], axis=1)


def pair_add(first, second):
    total = first[0] + second[0]
    backed = total - first[0]
    error = first[0] - (total - backed) + (second[0] - backed)
    error = error + first[1] + second[1]
    upper = total + error
    lower = error - (upper - total)
    return (upper, lower)


def tree_total(uppers, lowers):
    while uppers.shape[0] > 1:
        if uppers.shape[0] % 2 == 1:
            uppers = jnp.concatenate([uppers, jnp.zeros((1,), uppers.dtype)])
            lowers = jnp.concatenate([lowers, jnp.zeros((1,), lowers.dtype)])
        uppers, lowers = pair_add((uppers[0::2], lowers[0::2]), (uppers[1::2], lowers[1::2]))
    return (uppers[0], lowers[0])


def per_device(forcing, guess, shift, ocean_mask):
    mask_f = ocean_mask.astype(jnp.float32)
    theta = (HIGH_BOUND + LOW_BOUND) / 2.0
    delta = (HIGH_BOUND - LOW_BOUND) / 2.0
    sigma = theta / delta
    rho = 1.0 / sigma
    full = deep_inputs(forcing, guess, shift, mask_f)
    forcing_full = full[0]
    guess_full = full[1]
    shift_full = full[2]
    mask_full = full[3]
    iterate = mask_full * guess_full
    resid = crop_cycle(mask_full * forcing_full, 1) - local_stencil(iterate, shift_full, mask_full)
    direction = resid / theta
    iterate = crop_cycle(iterate, 1)
    for sweep in range(ITERS):
        iterate = iterate + direction
        image = local_stencil(direction, shift_full, mask_full)
        resid = crop_cycle(resid, 1) - image
        rho_next = 1.0 / (2.0 * sigma - rho)
        direction = rho_next * rho * crop_cycle(direction, 1) + 2.0 * rho_next / delta * resid
        rho = rho_next
        iterate = crop_cycle(iterate, 1)
    row_sums = jnp.sum(resid * resid, axis=1)
    upper, lower = tree_total(row_sums, jnp.zeros_like(row_sums))
    all_upper, all_lower = gather_turned((upper[None], lower[None]), ("bx", "by"), (0, 0))
    upper, lower = tree_total(all_upper, all_lower)
    grid_cells = resid.shape[0] * lax.axis_size("by") * resid.shape[1] * lax.axis_size("bx")
    norm_value = jnp.sqrt((upper + lower) / grid_cells)
    return (iterate, resid, norm_value)


def solution(mesh):
    in_specs = (P("by", "bx"), P("by", "bx"), P("by", "bx"), P("by", "bx"))
    out_specs = (P("by", "bx"), P("by", "bx"), P())
    return jax.shard_map(
        per_device, mesh=mesh, in_specs=in_specs, out_specs=out_specs, check_vma=False
    )
```

profile of v0, /device:TPU:1, one launch (start us, length us, event | category | flops | bytes accessed | tf_op | source)
XLA Modules:
  0.0 117.5 jit_solution(8575989142189107592)
XLA Ops:
  0.6 1.1 stack.15
  1.8 0.8 copy-done.1
  2.7 0.8 copy-done.2
  3.7 0.6 pad_maximum_fusion.1
  4.3 0.2 fusion.39
  4.5 2.2 %collective-permute-start = (f32[4,152,5]{2,0,1:T(4,128)S(1)}, f32[4,152,5]{2,0,1:T(4,128)S(1)}, u32[]{:S(2)}, u32[]{:S(2)}) collective-permute-start(f32[4,152,5]{2,0,1:T(4,128)S(1)} %get-tuple-element.75), channel_id=1, source_target_pairs={{0,16},{16,32},{32,48},{48,64},{64,80},{80,96},{96,112},{112,128},... | collective-permute-start | bytes 36488 | tf_op jit(solution)/shard_map/ppermute | solution.py:17
  6.7 3.7 %collective-permute-start.1 = (f32[4,152,5]{2,0,1:T(4,128)S(1)}, f32[4,152,5]{2,0,1:T(4,128)S(1)}, u32[]{:S(2)}, u32[]{:S(2)}) collective-permute-start(f32[4,152,5]{2,0,1:T(4,128)S(1)} %get-tuple-element.76), channel_id=1, source_target_pairs={{16,0},{32,16},{48,32},{64,48},{80,64},{96,80},{112,96},{128,112},... | collective-permute-start | bytes 36488 | tf_op jit(solution)/shard_map/ppermute | solution.py:20
  10.4 0.8 broadcast_in_dim.7
  11.2 3.5 %all-to-all-start = ((f32[16,4,5,256]{3,1,2,0:T(4,128)}), f32[16,4,5,256]{3,1,2,0:T(4,128)S(1)}, u32[]{:S(2)}, u32[]{:S(2)}) async-start(f32[16,4,5,256]{3,1,2,0:T(4,128)} %broadcast_in_dim.7), calls=%async_computation | async-start | bytes 655360 | tf_op jit(solution)/shard_map/all_to_all | solution.py:27
  14.8 0.8 collective-permute-done
  15.5 0.2 pad_maximum_fusion.7
  15.8 6.2 %collective-permute-start.2 = (f32[4,5,266]{2,0,1:T(4,128)S(1)}, f32[4,5,266]{2,0,1:T(4,128)S(1)}, u32[]{:S(2)}, u32[]{:S(2)}) collective-permute-start(f32[4,5,266]{2,0,1:T(4,128)S(1)} %get-tuple-element.69), channel_id=1, source_target_pairs={{0,1},{1,2},{2,3},{3,4},{4,5},{5,6},{6,7},{7,8},{8,9},{9,10},{10,1... | collective-permute-start | bytes 63848 | tf_op jit(solution)/shard_map/ppermute | solution.py:17
  22.0 1.0 collective-permute-done.2
  23.1 3.1 %rev.3 = f32[4,5,4096]{2,0,1:T(4,128)S(1)} reverse(f32[4,5,4096]{2,0,1:T(4,128)S(1)} %bitcast.28), dimensions={1,2} | reverse | bytes 655360 | tf_op jit(solution)/shard_map/rev | solution.py:75
  26.3 0.4 concatenate.31
  26.9 2.3 %pad_maximum_fusion = f32[4,162,266]{2,0,1:T(4,128)S(1)} fusion(f32[4,5,266]{2,0,1:T(4,128)S(1)} %dynamic-slice_select_fusion, f32[4,152,5]{2,0,1:T(4,128)S(1)} %collective-permute-done.1, f32[1,152,256]{2,0,1:T(1,128)S(1)} %stack.18, f32[1,152,256]{2,0,1:T(1,128)S(1)} %stack.17, f32[1,152,256]{2,0,1:T(1,128)S(1)} %stack.16, f32[1,152,256]{2,0,1:T(1,128)S(1)} %stack.15, ...), kind=kLoop, calls=%fused_computation | loop fusion | flops 1206576 | bytes 1378944 | tf_op jit(solution)/shard_map/concatenate | solution.py:81
  29.2 0.7 fusion.38
  30.2 0.7 broadcast_multiply_fusion
  31.0 0.6 multiply_add_fusion.2
  31.8 0.6 multiply_add_fusion.1
  32.4 0.6 multiply_add_fusion
  33.1 1.4 %multiply_reduce_fusion = (f32[152]{0:T(256)S(1)}, f32[152,256]{1,0:T(8,128)}, f32[152,256]{1,0:T(8,128)}) fusion(f32[154,258]{1,0:T(8,128)S(1)} %get-tuple-element.61, f32[162,266]{1,0:T(8,128)S(1)} %bitcast.26, f32[162,266]{1,0:T(8,128)S(1)} %get-tuple-element.90, f32[154,258]{1,0:T(8,128)S(1)} %get-tuple-element.62, f32[154,258]{1,0:T(8,128)S(1)} %get-tuple-element.80, ...), kind=kLoop, calls=%fused_computation.80 | loop fusion | flops 739176 | bytes 2802272 | tf_op jit(solution)/shard_map/reduce_sum | solution.py:126
  38.0 0.6 fusion.44
  41.0 0.6 fusion.43
  43.5 63.3 %all-gather = f32[256,1,2]{2,1,0:T(1,128)S(1)} all-gather(f32[1,1,2]{2,1,0:T(1,128)S(1)} %maximum_bitcast_fusion), channel_id=1, replica_groups=mesh['bx'=16,'by'=16] {'bx','by'}, dimensions={0}, use_global_device_ids=true | all-gather | bytes 2056 | tf_op jit(solution)/shard_map/all_gather | solution.py:44
  106.8 0.2 slice_reduce_fusion
  107.1 0.2 slice.547
  107.3 0.2 slice.546
  107.5 0.2 slice.544
  107.7 0.2 slice.543
  110.9 0.6 fusion.42
  113.9 0.6 fusion.41
  (110 shorter events, 7.6 us)
Async XLA Ops:
  0.6 1.1 copy-start
  1.7 0.9 copy-start.1
  2.6 0.9 copy-start.2
  4.5 11.0 %collective-permute-start = (f32[4,152,5]{2,0,1:T(4,128)S(1)}, f32[4,152,5]{2,0,1:T(4,128)S(1)}, u32[]{:S(2)}, u32[]{:S(2)}) collective-permute-start(f32[4,152,5]{2,0,1:T(4,128)S(1)} %get-tuple-element.75), channel_id=1, source_target_pairs={{0,16},{16,32},{32,48},{48,64},{64,80},{80,96},{96,112},{112,128},... | collective-permute-start | bytes 36488 | tf_op jit(solution)/shard_map/ppermute | solution.py:17
  6.7 8.9 %collective-permute-start.1 = (f32[4,152,5]{2,0,1:T(4,128)S(1)}, f32[4,152,5]{2,0,1:T(4,128)S(1)}, u32[]{:S(2)}, u32[]{:S(2)}) collective-permute-start(f32[4,152,5]{2,0,1:T(4,128)S(1)} %get-tuple-element.76), channel_id=1, source_target_pairs={{16,0},{32,16},{48,32},{64,48},{80,64},{96,80},{112,96},{128,112},... | collective-permute-start | bytes 36488 | tf_op jit(solution)/shard_map/ppermute | solution.py:20
  11.2 11.7 %all-to-all-start = ((f32[16,4,5,256]{3,1,2,0:T(4,128)}), f32[16,4,5,256]{3,1,2,0:T(4,128)S(1)}, u32[]{:S(2)}, u32[]{:S(2)}) async-start(f32[16,4,5,256]{3,1,2,0:T(4,128)} %broadcast_in_dim.7), calls=%async_computation | async-start | bytes 655360 | tf_op jit(solution)/shard_map/all_to_all | solution.py:27
  15.8 7.2 %collective-permute-start.2 = (f32[4,5,266]{2,0,1:T(4,128)S(1)}, f32[4,5,266]{2,0,1:T(4,128)S(1)}, u32[]{:S(2)}, u32[]{:S(2)}) collective-permute-start(f32[4,5,266]{2,0,1:T(4,128)S(1)} %get-tuple-element.69), channel_id=1, source_target_pairs={{0,1},{1,2},{2,3},{3,4},{4,5},{5,6},{6,7},{7,8},{8,9},{9,10},{10,1... | collective-permute-start | bytes 63848 | tf_op jit(solution)/shard_map/ppermute | solution.py:17
  22.0 4.8 %collective-permute-start.3 = (f32[4,5,266]{2,0,1:T(4,128)S(1)}, f32[4,5,266]{2,0,1:T(4,128)S(1)}, u32[]{:S(2)}, u32[]{:S(2)}) collective-permute-start(f32[4,5,266]{2,0,1:T(4,128)S(1)} %get-tuple-element.70), channel_id=1, source_target_pairs={{1,0},{2,1},{3,2},{4,3},{5,4},{6,5},{7,6},{8,7},{9,8},{10,9},{11,1... | collective-permute-start | bytes 63848 | tf_op jit(solution)/shard_map/ppermute | solution.py:20
where the time goes:
time: 118 us
  blocking collectives  63.3 us (54%)
  local copies, waits for them, and re-layouts  17.9 us (15%)
  starting transfers between devices  15.7 us (13%)
  between operations  10.8 us (9%)
  other arithmetic  8.12 us (7%)
  waiting for transfers between devices  1.77 us (2%)
    all_gather x1, blocking collectives, gather_turned(): filled, at, outs = (lax.all_gather(both, axis, axis=0, tiled=True), 0, [])  63.3 us
    ppermute x2, starting transfers between devices, padded_2(): lax.ppermute(lax.slice_in_dim(block, block.shape[dim] - width, None, axis...  8.39 us
    ppermute x2, starting transfers between devices, padded_2(): lax.ppermute(lax.slice_in_dim(block, 0, width, axis=dim), axis, backward)  3.73 us
    all_to_all x1, starting transfers between devices, sent_to_all(): return lax.all_to_all(copies, axis, split_axis=0, concat_axis=0, tiled=True)  3.54 us
    rev x1, local copies, waits for them, and re-layouts, deep_inputs(): flipped = whole_top[:, ::-1, ::-1]  3.06 us
    slice x16, local copies, waits for them, and re-layouts, tree_total(): uppers[1::2]  2.87 us
    slice x15, local copies, waits for them, and re-layouts, tree_total(): lowers[1::2]  2.7 us
  transfers between devices with their start and end apart: 5, of which 2 were waited for; matrix products, arithmetic and copies ran while one was open for 4% of the time, Pallas kernels for 0%

commit v1 on v0

--- a/solution.py
+++ b/solution.py
@@ -41,7 +41,16 @@
 def gather_turned(arrays, axis, dims):
     turned = [jnp.moveaxis(a, dim, 0) for a, dim in zip(arrays, dims)]
     both = jnp.concatenate([t.reshape(len(t), -1) for t in turned], axis=1)
-    filled, at, outs = (lax.all_gather(both, axis, axis=0, tiled=True), 0, [])
+    compute_quarters = lambda raw, comm_axis: jnp.concatenate(
+        lax.all_to_all(
+            jnp.stack([raw for _ in range(lax.axis_size(comm_axis))], 0),
+            concat_axis=0,
+            split_axis=0,
+            axis_name=comm_axis,
+        ),
+        0,
+    )
+    filled, at, outs = (compute_quarters(both, axis), 0, [])
     for t, dim in zip(turned, dims):
         piece = filled[:, at : at + t[0].size].reshape(-1, *t.shape[1:])
         outs.append(jnp.moveaxis(piece, 0, dim))

time: 118 us -> 84.7 us (0.72)
  blocking collectives: 63.3 us -> 30 us
    all_gather x1 -> x0, blocking collectives: 63.3 us -> none  [gather_turned(): filled, at, outs = (lax.all_gather(both, axis, axis=0, tiled=True), 0, [])]
    all_to_all x0 -> x1, blocking collectives: none -> 30 us  [gather_turned(): lax.all_to_all(jnp.stack([raw for _ in range(lax.axis_size(comm_axis))],...]
  transfers between devices with their start and end apart: 5 -> 5, of which waited for: 2 -> 2; matrix products, arithmetic and copies ran while one was open for 4% -> 6% of each run, Pallas kernels for 0% -> 0%
where the time goes in v1:
time: 84.7 us; the launch traced here: 84.3 us
  blocking collectives  30 us (35%)
  local copies, waits for them, and re-layouts  18 us (21%)
  starting transfers between devices  15.7 us (19%)
  between operations  10.8 us (13%)
  other arithmetic  8.12 us (10%)
  waiting for transfers between devices  1.77 us (2%)
    all_to_all x1, blocking collectives, gather_turned(): lax.all_to_all(jnp.stack([raw for _ in range(lax.axis_size(comm_axis))],...  30 us
    ppermute x2, starting transfers between devices, padded_2(): lax.ppermute(lax.slice_in_dim(block, block.shape[dim] - width, None, axis...  8.39 us
    ppermute x2, starting transfers between devices, padded_2(): lax.ppermute(lax.slice_in_dim(block, 0, width, axis=dim), axis, backward)  3.73 us
    all_to_all x1, starting transfers between devices, sent_to_all(): return lax.all_to_all(copies, axis, split_axis=0, concat_axis=0, tiled=True)  3.54 us
    rev x1, local copies, waits for them, and re-layouts, deep_inputs(): flipped = whole_top[:, ::-1, ::-1]  3.06 us
    slice x16, local copies, waits for them, and re-layouts, tree_total(): uppers[1::2]  2.87 us
    slice x15, local copies, waits for them, and re-layouts, tree_total(): lowers[1::2]  2.7 us
    concatenate x1, other arithmetic, deep_inputs(): jnp.concatenate([lower_rows, padded[:, depth:rows + depth], upper_rows],...  2.33 us
  transfers between devices with their start and end apart: 5, of which 2 were waited for; matrix products, arithmetic and copies ran while one was open for 6% of the time, Pallas kernels for 0%

profile of v1, /device:TPU:1, one launch (start us, length us, event | category | flops | bytes accessed | tf_op | source)
XLA Modules:
  0.0 84.3 jit_solution(11696094138121313663)
XLA Ops:
  0.6 1.1 %stack.12 = f32[1,152,256]{2,0,1:T(1,128)S(1)} reshape(f32[152,256]{1,0:T(8,128)} %param.4) | data formatting | bytes 311296 | tf_op jit(solution)/shard_map/stack | solution.py:80
  1.8 0.8 copy-done.1
  2.7 0.8 copy-done.2
  3.7 0.6 pad_maximum_fusion.1
  4.3 0.2 fusion.39
  4.5 2.2 %collective-permute-start = (f32[4,152,5]{2,0,1:T(4,128)S(1)}, f32[4,152,5]{2,0,1:T(4,128)S(1)}, u32[]{:S(2)}, u32[]{:S(2)}) collective-permute-start(f32[4,152,5]{2,0,1:T(4,128)S(1)} %get-tuple-element.75), channel_id=1, source_target_pairs={{0,16},{16,32},{32,48},{48,64},{64,80},{80,96},{96,112},{112,128},... | collective-permute-start | bytes 36488 | tf_op jit(solution)/shard_map/ppermute | solution.py:17
  6.7 3.7 %collective-permute-start.1 = (f32[4,152,5]{2,0,1:T(4,128)S(1)}, f32[4,152,5]{2,0,1:T(4,128)S(1)}, u32[]{:S(2)}, u32[]{:S(2)}) collective-permute-start(f32[4,152,5]{2,0,1:T(4,128)S(1)} %get-tuple-element.76), channel_id=1, source_target_pairs={{16,0},{32,16},{48,32},{64,48},{80,64},{96,80},{112,96},{128,112},... | collective-permute-start | bytes 36488 | tf_op jit(solution)/shard_map/ppermute | solution.py:20
  10.4 0.8 broadcast_in_dim.7
  11.2 3.5 %all-to-all-start = ((f32[16,4,5,256]{3,1,2,0:T(4,128)}), f32[16,4,5,256]{3,1,2,0:T(4,128)S(1)}, u32[]{:S(2)}, u32[]{:S(2)}) async-start(f32[16,4,5,256]{3,1,2,0:T(4,128)} %broadcast_in_dim.7), calls=%async_computation | async-start | bytes 655360 | tf_op jit(solution)/shard_map/all_to_all | solution.py:27
  14.8 0.8 collective-permute-done
  15.5 0.2 pad_maximum_fusion.7
  15.8 6.2 %collective-permute-start.2 = (f32[4,5,266]{2,0,1:T(4,128)S(1)}, f32[4,5,266]{2,0,1:T(4,128)S(1)}, u32[]{:S(2)}, u32[]{:S(2)}) collective-permute-start(f32[4,5,266]{2,0,1:T(4,128)S(1)} %get-tuple-element.69), channel_id=1, source_target_pairs={{0,1},{1,2},{2,3},{3,4},{4,5},{5,6},{6,7},{7,8},{8,9},{9,10},{10,1... | collective-permute-start | bytes 63848 | tf_op jit(solution)/shard_map/ppermute | solution.py:17
  22.0 1.0 %collective-permute-done.2 = f32[4,5,266]{2,0,1:T(4,128)S(1)} collective-permute-done((f32[4,5,266]{2,0,1:T(4,128)S(1)}, f32[4,5,266]{2,0,1:T(4,128)S(1)}, u32[]{:S(2)}, u32[]{:S(2)}) %collective-permute-start.2) | collective-permute-done | bytes 21312 | tf_op jit(solution)/shard_map/ppermute | solution.py:17
  23.1 3.1 %rev.3 = f32[4,5,4096]{2,0,1:T(4,128)S(1)} reverse(f32[4,5,4096]{2,0,1:T(4,128)S(1)} %bitcast.28), dimensions={1,2} | reverse | bytes 655360 | tf_op jit(solution)/shard_map/rev | solution.py:84
  26.3 0.4 concatenate.33
  26.9 2.3 %pad_maximum_fusion = f32[4,162,266]{2,0,1:T(4,128)S(1)} fusion(f32[4,5,266]{2,0,1:T(4,128)S(1)} %dynamic-slice_select_fusion, f32[4,152,5]{2,0,1:T(4,128)S(1)} %collective-permute-done.1, f32[1,152,256]{2,0,1:T(1,128)S(1)} %stack.15, f32[1,152,256]{2,0,1:T(1,128)S(1)} %stack.14, f32[1,152,256]{2,0,1:T(1,128)S(1)} %stack.13, f32[1,152,256]{2,0,1:T(1,128)S(1)} %stack.12, ...), kind=kLoop, calls=%fused_computation | loop fusion | flops 1206576 | bytes 1378944 | tf_op jit(solution)/shard_map/concatenate | solution.py:90
  29.2 0.7 fusion.38
  30.2 0.7 broadcast_multiply_fusion
  31.0 0.6 multiply_add_fusion.2
  31.8 0.6 multiply_add_fusion.1
  32.4 0.6 multiply_add_fusion
  33.1 1.4 %multiply_reduce_fusion = (f32[152]{0:T(256)S(1)}, f32[152,256]{1,0:T(8,128)}, f32[152,256]{1,0:T(8,128)}) fusion(f32[154,258]{1,0:T(8,128)S(1)} %get-tuple-element.61, f32[162,266]{1,0:T(8,128)S(1)} %bitcast.26, f32[162,266]{1,0:T(8,128)S(1)} %get-tuple-element.90, f32[154,258]{1,0:T(8,128)S(1)} %get-tuple-element.62, f32[154,258]{1,0:T(8,128)S(1)} %get-tuple-element.80, ...), kind=kLoop, calls=%fused_computation.80 | loop fusion | flops 739176 | bytes 2802272 | tf_op jit(solution)/shard_map/reduce_sum | solution.py:135
  38.0 0.6 fusion.44
  41.0 0.6 fusion.43
  43.6 30.0 %all_to_all.10 = f32[256,1,2]{2,1,0:T(1,128)S(1)} all-to-all(f32[256,1,2]{2,1,0:T(1,128)S(1)} %stack.17), channel_id=1, replica_groups=mesh['bx'=16,'by'=16] {'bx','by'}, dimensions={0} | all-to-all | bytes 4096 | tf_op jit(solution)/shard_map/all_to_all | solution.py:45
  73.6 0.2 slice_reduce_fusion
  73.9 0.2 slice.547
  74.1 0.2 slice.546
  74.3 0.2 slice.544
  74.5 0.2 slice.543
  77.7 0.6 fusion.42
  80.7 0.6 fusion.41
  (111 shorter events, 7.7 us)
Async XLA Ops:
  0.6 1.1 %copy-start = (f32[152,256]{1,0:T(8,128)S(1)}, f32[152,256]{1,0:T(8,128)}, u32[]{:S(2)}) copy-start(f32[152,256]{1,0:T(8,128)} %param.5) | copy-start | bytes 466948
  1.7 0.9 %copy-start.1 = (f32[152,256]{1,0:T(8,128)S(1)}, f32[152,256]{1,0:T(8,128)}, u32[]{:S(2)}) copy-start(f32[152,256]{1,0:T(8,128)} %param.6) | copy-start | bytes 466948
  2.6 0.9 %copy-start.2 = (s32[152,256]{1,0:T(8,128)S(1)}, s32[152,256]{1,0:T(8,128)}, u32[]{:S(2)}) copy-start(s32[152,256]{1,0:T(8,128)} %param.7) | copy-start | bytes 466948
  4.5 11.0 %collective-permute-start = (f32[4,152,5]{2,0,1:T(4,128)S(1)}, f32[4,152,5]{2,0,1:T(4,128)S(1)}, u32[]{:S(2)}, u32[]{:S(2)}) collective-permute-start(f32[4,152,5]{2,0,1:T(4,128)S(1)} %get-tuple-element.75), channel_id=1, source_target_pairs={{0,16},{16,32},{32,48},{48,64},{64,80},{80,96},{96,112},{112,128},... | collective-permute-start | bytes 36488 | tf_op jit(solution)/shard_map/ppermute | solution.py:17
  6.7 8.9 %collective-permute-start.1 = (f32[4,152,5]{2,0,1:T(4,128)S(1)}, f32[4,152,5]{2,0,1:T(4,128)S(1)}, u32[]{:S(2)}, u32[]{:S(2)}) collective-permute-start(f32[4,152,5]{2,0,1:T(4,128)S(1)} %get-tuple-element.76), channel_id=1, source_target_pairs={{16,0},{32,16},{48,32},{64,48},{80,64},{96,80},{112,96},{128,112},... | collective-permute-start | bytes 36488 | tf_op jit(solution)/shard_map/ppermute | solution.py:20
  11.2 11.7 %all-to-all-start = ((f32[16,4,5,256]{3,1,2,0:T(4,128)}), f32[16,4,5,256]{3,1,2,0:T(4,128)S(1)}, u32[]{:S(2)}, u32[]{:S(2)}) async-start(f32[16,4,5,256]{3,1,2,0:T(4,128)} %broadcast_in_dim.7), calls=%async_computation | async-start | bytes 655360 | tf_op jit(solution)/shard_map/all_to_all | solution.py:27
  15.8 7.2 %collective-permute-start.2 = (f32[4,5,266]{2,0,1:T(4,128)S(1)}, f32[4,5,266]{2,0,1:T(4,128)S(1)}, u32[]{:S(2)}, u32[]{:S(2)}) collective-permute-start(f32[4,5,266]{2,0,1:T(4,128)S(1)} %get-tuple-element.69), channel_id=1, source_target_pairs={{0,1},{1,2},{2,3},{3,4},{4,5},{5,6},{6,7},{7,8},{8,9},{9,10},{10,1... | collective-permute-start | bytes 63848 | tf_op jit(solution)/shard_map/ppermute | solution.py:17
  22.0 4.8 %collective-permute-start.3 = (f32[4,5,266]{2,0,1:T(4,128)S(1)}, f32[4,5,266]{2,0,1:T(4,128)S(1)}, u32[]{:S(2)}, u32[]{:S(2)}) collective-permute-start(f32[4,5,266]{2,0,1:T(4,128)S(1)} %get-tuple-element.70), channel_id=1, source_target_pairs={{1,0},{2,1},{3,2},{4,3},{5,4},{6,5},{7,6},{8,7},{9,8},{10,9},{11,1... | collective-permute-start | bytes 63848 | tf_op jit(solution)/shard_map/ppermute | solution.py:20
